TPU v7x, 32 devices: a whole 2x2x4 slice. The times are simulated.
32 devices in a mesh: rep: 2 (over x), dp: 16 (over y, z, core).
Axes of the slice: x: 2, y: 2, z: 4, core: 2. Of those that a mesh axis runs over, the one named last changes fastest.
Arguments:
- x: bfloat16 [32, 2048, 1024], P(('rep', 'dp')), parts along dimension 0
- dy: bfloat16 [32, 2048, 1024], P(('rep', 'dp')), parts along dimension 0
- w_gate: bfloat16 [2, 1024, 2816], P(None, 'dp')
- w_up: bfloat16 [2, 1024, 2816], P(None, 'dp')
- w_down: bfloat16 [2, 2816, 1024], P(None, 'dp')
Outputs:
- output 1: bfloat16 [32, 2048, 1024], P(('rep', 'dp')), parts along dimension 0
- output 2: bfloat16 [4, 1024, 2816], P('rep', 'dp'), parts along dimension 0
- output 3: bfloat16 [4, 1024, 2816], P('rep', 'dp'), parts along dimension 0
- output 4: bfloat16 [4, 2816, 1024], P('rep', 'dp'), parts along dimension 0
There are 2 independent parts. A program takes and returns all parts, laid end to end along the dimension named above; an argument that names none is the same for every part.
All inputs are finite; a program needn't handle non-finite values.
Results may differ from a plain program's by a relative error of at most 0.018.
Values are sent between devices in bfloat16 or wider.
A program may use at most 2 GiB of HBM per device.

v0:
```python
import jax
import jax.numpy as jnp
from jax import lax

NAMES = ("w_gate", "w_up", "w_down")


def matmul(a, w):
    return jnp.dot(a, w, preferred_element_type=jnp.float32).astype(jnp.bfloat16)


def normed(h):
    wide = h.astype(jnp.float32)
    scale = lax.rsqrt(jnp.mean(wide**2, -1, keepdims=True) + 1e-6)
    return (wide * scale).astype(jnp.bfloat16)


def layer(h, w):
    a = normed(h)
    gate = jnp.dot(a, w["w_gate"], preferred_element_type=jnp.float32)
    up = jnp.dot(a, w["w_up"], preferred_element_type=jnp.float32)
    return h + matmul((jax.nn.silu(gate) * up).astype(jnp.bfloat16), w["w_down"])


def stack(weights, h):
    for number in range(weights["w_gate"].shape[0]):
        h = layer(h, {name: w[number] for name, w in weights.items()})
    return h


def solution(mesh):
    groups = mesh.shape["rep"]

    def step(x, dy, *weights):
        shape = x.shape
        x, dy = (t.reshape(groups, -1, *t.shape[1:]) for t in (x, dy))

        def of_a_group(x, dy):
            _, back = jax.vjp(stack, dict(zip(NAMES, weights, strict=True)), x)
            by_weights, by_x = back(dy)
            return (by_x, *(by_weights[name] for name in NAMES))

        by_x, *by_weights = jax.vmap(of_a_group)(x, dy)
        return (by_x.reshape(shape), *(t.reshape(-1, *t.shape[2:]) for t in by_weights))

    return step
```

profile of v0, /device:TPU:6, one launch (start us, length us, event | category | flops | bytes accessed | tf_op | source)
XLA Modules:
  0.0 1622.9 jit_solution(17147968810204355008)
XLA Ops:
  38.4 30.8 %all-gather.30.cloned.1.call-done = bf16[1,1024,2816]{2,1,0:T(8,128)(2,1)} async-done(((bf16[1,64,2816]{2,1,0:T(8,128)(2,1)}), bf16[1,1024,2816]{2,1,0:T(8,128)(2,1)}) %all-gather.30.cloned.1.call-update) | async-done | bytes 5767184 | tf_op jit(solution)/vmap(jvp())/squeeze | solution.py:27
  69.3 19.8 %fusion.190 = f32[2048,2816]{1,0:T(8,128)} fusion(bf16[1,1024,2816]{2,1,0:T(8,128)(2,1)} %all-gather.30.cloned.1.call-done, bf16[1,2048,1024]{2,1,0:T(8,128)(2,1)} %param.13, f32[2048]{0:T(1024)S(1)} %get-tuple-element.267), kind=kOutput, calls=%fused_computation.241 | convolution fusion | flops 11817451520 | bytes 33038336 | tf_op jit(solution)/vmap(jvp())/dot_general | solution.py:20
  89.0 39.9 %all-gather.32.cloned.1.call-done = bf16[1,1024,2816]{2,1,0:T(8,128)(2,1)} async-done(((bf16[1,64,2816]{2,1,0:T(8,128)(2,1)}), bf16[1,1024,2816]{2,1,0:T(8,128)(2,1)}) %all-gather.32.cloned.1.call-update) | async-done | bytes 5767184 | tf_op jit(solution)/vmap(jvp())/squeeze | solution.py:27
  128.9 28.7 %fusion.160 = (bf16[1,1,2048,2816]{3,2,1,0:T(8,128)(2,1)}, f32[2048,2816]{1,0:T(8,128)}) fusion(f32[2048,2816]{1,0:T(8,128)} %fusion.190, bf16[1,1024,2816]{2,1,0:T(8,128)(2,1)} %all-gather.32.cloned.1.call-done, bf16[1,2048,1024]{2,1,0:T(8,128)(2,1)} %param.13, f32[2048]{0:T(1024)S(1)} %get-tuple-element.267), kind=kOutput, calls=%fused_computation.195 | convolution fusion | flops 11852054528 | bytes 67641344 | tf_op jit(solution)/vmap(jvp())/dot_general | solution.py:21
  157.7 31.0 %all-gather.34.cloned.1.call-done = bf16[1,2816,1024]{2,1,0:T(8,128)(2,1)} async-done(((bf16[1,176,1024]{2,1,0:T(8,128)(2,1)}), bf16[1,2816,1024]{2,1,0:T(8,128)(2,1)}) %all-gather.34.cloned.1.call-update) | async-done | bytes 5767184 | tf_op jit(solution)/vmap(jvp())/squeeze | solution.py:27
  188.6 20.1 %fusion.174 = (f32[2048]{0:T(1024)S(1)}, bf16[1,1,2048,1024]{2,3,1,0:T(8,128)(2,1)}) fusion(bf16[1,2816,1024]{2,1,0:T(8,128)(2,1)} %all-gather.34.cloned.1.call-done, bf16[1,1,2048,2816]{3,2,1,0:T(8,128)(2,1)} %get-tuple-element.268, bf16[1,2048,1024]{1,2,0:T(8,128)(2,1)} %copy.1), kind=kOutput, calls=%fused_computation.225 | convolution fusion | flops 11821643776 | bytes 25698304 | tf_op jit(solution)/vmap(jvp())/dot_general | solution.py:9
  215.4 32.8 %all-gather.36.cloned.1.call-done = bf16[1,1024,2816]{2,1,0:T(8,128)(2,1)} async-done(((bf16[1,64,2816]{2,1,0:T(8,128)(2,1)}), bf16[1,1024,2816]{2,1,0:T(8,128)(2,1)}) %all-gather.36.cloned.1.call-update) | async-done | bytes 5767184 | tf_op jit(solution)/vmap(jvp())/squeeze | solution.py:27
  248.2 20.1 %fusion.182 = f32[2048,2816]{1,0:T(8,128)} fusion(bf16[1,1024,2816]{2,1,0:T(8,128)(2,1)} %all-gather.36.cloned.1.call-done, bf16[1,1,2048,1024]{2,3,1,0:T(8,128)(2,1)} %fusion.175), kind=kOutput, calls=%fused_computation.233 | convolution fusion | flops 11811160064 | bytes 33030144 | tf_op jit(solution)/vmap(jvp())/dot_general | solution.py:20
  268.3 39.4 %all-gather.40.cloned.1.call-done = bf16[1,1024,2816]{2,1,0:T(8,128)(2,1)} async-done(((bf16[1,64,2816]{2,1,0:T(8,128)(2,1)}), bf16[1,1024,2816]{2,1,0:T(8,128)(2,1)}) %all-gather.40.cloned.1.call-update) | async-done | bytes 5767184 | tf_op jit(solution)/vmap(jvp())/squeeze | solution.py:27
  307.7 27.9 %fusion.154 = (bf16[1,1,2048,2816]{3,2,1,0:T(8,128)(2,1)}, f32[2048,2816]{1,0:T(8,128)}) fusion(f32[2048,2816]{1,0:T(8,128)} %fusion.182, bf16[1,1024,2816]{2,1,0:T(8,128)(2,1)} %all-gather.40.cloned.1.call-done, bf16[1,1,2048,1024]{2,3,1,0:T(8,128)(2,1)} %fusion.175), kind=kOutput, calls=%fused_computation.185 | convolution fusion | flops 11845763072 | bytes 67633152 | tf_op jit(solution)/vmap(jvp())/dot_general | solution.py:21
  335.6 15.1 copy.4
  350.7 15.1 copy.2
  365.8 170.5 %while.16 = (bf16[1,1,2048,2816]{2,3,1,0:T(8,128)(2,1)}, bf16[1,1,2048,1024]{3,2,1,0:T(8,128)(2,1)}, f32[1,176,1024]{2,1,0:T(8,128)S(1)}, f32[1,176,1024]{2,1,0:...) while((bf16[1,1,2048,2816]{2,3,1,0:T(8,128)(2,1)}, ...), condition=%wide.windowed_dot_general_cond_rs.4.clone, body=%wide.windowed_dot_general_body_rs.4.clone.sunk | while | flops 2959638528 | bytes 57410148 | solution.py:9
  536.3 33.9 %convert_multiply_fusion.3 = (bf16[1,1,2048,2816]{3,2,1,0:T(8,128)(2,1)}, bf16[1,1,2048,2816]{3,2,1,0:T(8,128)(2,1)}) fusion(f32[2048,2816]{1,0:T(8,128)} %fusion.182, f32[2048,2816]{1,0:T(8,128)} %get-tuple-element.276, bf16[1,2816,1024]{2,1,0:T(8,128)(2,1)} %all-gather.38.cloned.1.call-done, bf16[1,2048,1024]{2,1,0:T(8,128)(2,1)} %param.12), kind=kOutput, calls=%fused_computation.173 | convolution fusion | flops 11903434752 | bytes 79167488 | tf_op jit(solution)/vmap(transpose(jvp()))/dot_general | solution.py:9
  570.3 18.2 %fusion.152 = bf16[2048,1024]{0,1:T(8,128)(2,1)} fusion(bf16[1,1,2048,2816]{3,2,1,0:T(8,128)(2,1)} %get-tuple-element.551, bf16[1,1024,2816]{2,1,0:T(8,128)(2,1)} %all-gather.36.cloned.1.call-done), kind=kOutput, calls=%fused_computation.182 | convolution fusion | flops 11811160064 | bytes 21495808 | tf_op jit(solution)/vmap(transpose(jvp()))/dot_general | solution.py:20
  588.5 17.3 %fusion.176 = (f32[2048]{0:T(1024)S(1)}, bf16[2048,1024]{0,1:T(8,128)(2,1)}) fusion(bf16[1,1,2048,1024]{2,3,1,0:T(8,128)(2,1)} %get-tuple-element.271, bf16[2048,1024]{0,1:T(8,128)(2,1)} %fusion.152, bf16[1,1024,2816]{2,1,0:T(8,128)(2,1)} %all-gather.40.cloned.1.call-done, bf16[1,1,2048,2816]{3,2,1,0:T(8,128)(2,1)S(1)} %copy-done.4), kind=kOutput, calls=%fused_computation.227 | convolution fusion | flops 11821643776 | bytes 29892608 | tf_op jit(solution)/vmap(transpose(jvp()))/dot_general | solution.py:21
  619.4 171.7 %while.17 = (bf16[1,1,2048,2816]{2,3,1,0:T(8,128)(2,1)}, bf16[1,1,2048,1024]{3,2,1,0:T(8,128)(2,1)}, f32[1,176,1024]{2,1,0:T(8,128)S(1)}, f32[1,176,1024]{2,1,0:...) while((bf16[1,1,2048,2816]{2,3,1,0:T(8,128)(2,1)}, ...), condition=%wide.windowed_dot_general_cond_rs.5.clone, body=%wide.windowed_dot_general_body_rs.5.clone.sunk | while | flops 2959638528 | bytes 57410148 | solution.py:9
  792.0 185.7 %while.14 = (bf16[1,1,2048,1024]{2,3,1,0:T(8,128)(2,1)}, bf16[1,1,2048,2816]{3,2,1,0:T(8,128)(2,1)}, f32[1,64,2816]{2,1,0:T(8,128)}, f32[1,64,2816]{2,1,0:T(8,12...) while((bf16[1,1,2048,1024]{2,3,1,0:T(8,128)(2,1)}, ...), condition=%wide.windowed_dot_general_cond_rs.2.clone, body=%wide.windowed_dot_general_body_rs.2.clone.sunk | while | flops 2955968512 | bytes 108790480 | solution.py:21
  871.9 14.9 collective-permute-done.10
  962.4 14.1 collective-permute-done.10
  977.7 34.0 %convert_multiply_fusion.1 = (bf16[1,1,2048,2816]{3,2,1,0:T(8,128)(2,1)}, bf16[1,1,2048,2816]{3,2,1,0:T(8,128)(2,1)}) fusion(f32[2048,2816]{1,0:T(8,128)} %fusion.190, f32[2048,2816]{1,0:T(8,128)} %get-tuple-element.269, bf16[1,2816,1024]{2,1,0:T(8,128)(2,1)} %all-gather.34.cloned.1.call-done, bf16[1,1,2048,1024]{2,3,1,0:T(8,128)(2,1)} %fusion.194), kind=kOutput, calls=%fused_computation.171 | convolution fusion | flops 11903434752 | bytes 79167488 | tf_op jit(solution)/vmap(transpose(jvp()))/dot_general | solution.py:9
  1011.7 18.2 %fusion.148 = bf16[2048,1024]{0,1:T(8,128)(2,1)} fusion(bf16[1,1,2048,2816]{3,2,1,0:T(8,128)(2,1)} %get-tuple-element.512, bf16[1,1024,2816]{2,1,0:T(8,128)(2,1)} %all-gather.30.cloned.1.call-done), kind=kOutput, calls=%fused_computation.178 | convolution fusion | flops 11811160064 | bytes 21495808 | tf_op jit(solution)/vmap(transpose(jvp()))/dot_general | solution.py:20
  1029.9 18.5 %fusion.173 = (bf16[1,1,2048,1024]{2,3,1,0:T(8,128)(2,1)}, f32[2048]{0:T(1024)}, bf16[2048,1024]{0,1:T(8,128)(2,1)}) fusion(bf16[1,2048,1024]{1,2,0:T(8,128)(2,1)} %copy.1, f32[2048]{0:T(1024)S(1)} %bitcast.588, bf16[2048,1024]{0,1:T(8,128)(2,1)} %fusion.148, bf16[1,1024,2816]{2,1,0:T(8,128)(2,1)} %all-gather.32.cloned.1.call-done, ...), kind=kOutput, calls=%fused_computation.224 | convolution fusion | flops 11825838080 | bytes 34095104 | tf_op jit(solution)/vmap(transpose(jvp()))/dot_general | solution.py:21
  1048.4 178.6 %while.15 = (bf16[1,1,2048,1024]{2,3,1,0:T(8,128)(2,1)}, bf16[1,1,2048,2816]{3,2,1,0:T(8,128)(2,1)}, f32[1,64,2816]{2,1,0:T(8,128)}, f32[1,64,2816]{2,1,0:T(8,12...) while((bf16[1,1,2048,1024]{2,3,1,0:T(8,128)(2,1)}, ...), condition=%wide.windowed_dot_general_cond_rs.3.clone, body=%wide.windowed_dot_general_body_rs.3.clone.sunk | while | flops 2955968512 | bytes 108790480 | solution.py:21
  1077.2 13.9 collective-permute-done.14
  1227.0 175.9 %while.12 = (bf16[1,1,2048,1024]{2,3,1,0:T(8,128)(2,1)}, bf16[1,1,2048,2816]{3,2,1,0:T(8,128)(2,1)}, f32[1,64,2816]{2,1,0:T(8,128)}, f32[1,64,2816]{2,1,0:T(8,12...) while((bf16[1,1,2048,1024]{2,3,1,0:T(8,128)(2,1)}, ...), condition=%wide.windowed_dot_general_cond_rs.clone, body=%wide.windowed_dot_general_body_rs.clone.sunk | while | flops 2955968512 | bytes 108790480 | solution.py:20
  1253.7 14.2 collective-permute-done.2
  1342.9 14.1 collective-permute-done.2
  1387.9 13.7 collective-permute-done.2
  1402.9 176.2 %while.13 = (bf16[1,1,2048,1024]{2,3,1,0:T(8,128)(2,1)}, bf16[1,1,2048,2816]{3,2,1,0:T(8,128)(2,1)}, f32[1,64,2816]{2,1,0:T(8,128)}, f32[1,64,2816]{2,1,0:T(8,12...) while((bf16[1,1,2048,1024]{2,3,1,0:T(8,128)(2,1)}, ...), condition=%wide.windowed_dot_general_cond_rs.1.clone, body=%wide.windowed_dot_general_body_rs.1.clone.sunk | while | flops 2955968512 | bytes 108790480 | solution.py:20
  1474.9 13.8 collective-permute-done.6
  1519.6 13.7 collective-permute-done.6
  (606 shorter events, 983.8 us)
Async XLA Ops:
  7.2 62.1 %all-gather.30.cloned.1.call-start = ((), (), s32[]{:S(2)}) async-start(), calls=%async_computation | async-start | bytes 6127616 | tf_op jit(solution)/vmap(jvp())/squeeze | solution.py:27
  9.3 119.7 %all-gather.32.cloned.1.call-start = ((), (), s32[]{:S(2)}) async-start(), calls=%async_computation.1 | async-start | bytes 6127616 | tf_op jit(solution)/vmap(jvp())/squeeze | solution.py:27
  11.4 177.2 %all-gather.34.cloned.1.call-start = ((), (), s32[]{:S(2)}) async-start(), calls=%async_computation.2 | async-start | bytes 6127616 | tf_op jit(solution)/vmap(jvp())/squeeze | solution.py:27
  13.5 234.7 %all-gather.36.cloned.1.call-start = ((), (), s32[]{:S(2)}) async-start(), calls=%async_computation.3 | async-start | bytes 6127616 | tf_op jit(solution)/vmap(jvp())/squeeze | solution.py:27
  14.1 293.6 %all-gather.40.cloned.1.call-start = ((), (), s32[]{:S(2)}) async-start(), calls=%async_computation.5 | async-start | bytes 6127616 | tf_op jit(solution)/vmap(jvp())/squeeze | solution.py:27
  14.7 521.7 %all-gather.38.cloned.1.call-start = ((), (), s32[]{:S(2)}) async-start(), calls=%async_computation.4 | async-start | bytes 6127616 | tf_op jit(solution)/vmap(jvp())/squeeze | solution.py:27
  385.3 20.6 %collective-permute-start.18 = (f32[1,176,1024]{2,1,0:T(8,128)S(1)}, f32[1,176,1024]{2,1,0:T(8,128)S(1)}, u32[]{:S(2)}, u32[]{:S(2)}) collective-permute-start(f32[1,176,1024]{2,1,0:T(8,128)S(1)} %get-tuple-element.498), channel_id=41, source_target_pairs={{0,1},{1,2},{2,3},{3,4},{4,5},{5,6},{6,7},{7,8},{8,9},{9,10},{10,1... | collective-permute-start | bytes 2162696 | tf_op jit(solution)/vmap(transpose(jvp()))/dot_general | solution.py:9
  449.0 20.6 %collective-permute-start.16 = (f32[1,176,1024]{2,1,0:T(8,128)S(1)}, f32[1,176,1024]{2,1,0:T(8,128)S(1)}, u32[]{:S(2)}, u32[]{:S(2)}) collective-permute-start(f32[1,176,1024]{2,1,0:T(8,128)S(1)} %broadcast_select_fusion.32), channel_id=39, source_target_pairs={{0,1},{1,2},{2,3},{3,4},{4,5},{5,6},{6,7},{7,8},{8,9},{9,10},{10,1... | collective-permute-start | bytes 2162696 | tf_op jit(solution)/vmap(transpose(jvp()))/dot_general | solution.py:9
  469.8 20.5 %collective-permute-start.18 = (f32[1,176,1024]{2,1,0:T(8,128)S(1)}, f32[1,176,1024]{2,1,0:T(8,128)S(1)}, u32[]{:S(2)}, u32[]{:S(2)}) collective-permute-start(f32[1,176,1024]{2,1,0:T(8,128)S(1)} %get-tuple-element.498), channel_id=41, source_target_pairs={{0,1},{1,2},{2,3},{3,4},{4,5},{5,6},{6,7},{7,8},{8,9},{9,10},{10,1... | collective-permute-start | bytes 2162696 | tf_op jit(solution)/vmap(transpose(jvp()))/dot_general | solution.py:9
  492.7 21.2 %collective-permute-start.16 = (f32[1,176,1024]{2,1,0:T(8,128)S(1)}, f32[1,176,1024]{2,1,0:T(8,128)S(1)}, u32[]{:S(2)}, u32[]{:S(2)}) collective-permute-start(f32[1,176,1024]{2,1,0:T(8,128)S(1)} %broadcast_select_fusion.32), channel_id=39, source_target_pairs={{0,1},{1,2},{2,3},{3,4},{4,5},{5,6},{6,7},{7,8},{8,9},{9,10},{10,1... | collective-permute-start | bytes 2162696 | tf_op jit(solution)/vmap(transpose(jvp()))/dot_general | solution.py:9
  514.1 21.1 %collective-permute-start.18 = (f32[1,176,1024]{2,1,0:T(8,128)S(1)}, f32[1,176,1024]{2,1,0:T(8,128)S(1)}, u32[]{:S(2)}, u32[]{:S(2)}) collective-permute-start(f32[1,176,1024]{2,1,0:T(8,128)S(1)} %get-tuple-element.498), channel_id=41, source_target_pairs={{0,1},{1,2},{2,3},{3,4},{4,5},{5,6},{6,7},{7,8},{8,9},{9,10},{10,1... | collective-permute-start | bytes 2162696 | tf_op jit(solution)/vmap(transpose(jvp()))/dot_general | solution.py:9
  514.2 21.0 %collective-permute-start.19 = (f32[1,176,1024]{2,1,0:T(8,128)S(1)}, f32[1,176,1024]{2,1,0:T(8,128)S(1)}, u32[]{:S(2)}, u32[]{:S(2)}) collective-permute-start(f32[1,176,1024]{2,1,0:T(8,128)S(1)} %get-tuple-element.499), channel_id=40, source_target_pairs={{0,15},{1,0},{2,1},{3,2},{4,3},{5,4},{6,5},{7,6},{8,7},{9,8},{10,9... | collective-permute-start | bytes 2162696 | tf_op jit(solution)/vmap(transpose(jvp()))/dot_general | solution.py:9
  536.3 1056.9 %collective-permute-start.28 = (f32[1,176,1024]{2,1,0:T(8,128)}, f32[1,176,1024]{2,1,0:T(8,128)}, u32[]{:S(2)}, u32[]{:S(2)}) collective-permute-start(f32[1,176,1024]{2,1,0:T(8,128)} %get-tuple-element.45), channel_id=42, source_target_pairs={{0,1},{1,2},{2,3},{3,4},{4,5},{5,6},{6,7},{7,8},{8,9},{9,10},{10,1... | collective-permute-start | bytes 2162696 | tf_op jit(solution)/vmap(transpose(jvp()))/dot_general | solution.py:9
  640.1 20.6 %collective-permute-start.22 = (f32[1,176,1024]{2,1,0:T(8,128)S(1)}, f32[1,176,1024]{2,1,0:T(8,128)S(1)}, u32[]{:S(2)}, u32[]{:S(2)}) collective-permute-start(f32[1,176,1024]{2,1,0:T(8,128)S(1)} %get-tuple-element.507), channel_id=47, source_target_pairs={{0,1},{1,2},{2,3},{3,4},{4,5},{5,6},{6,7},{7,8},{8,9},{9,10},{10,1... | collective-permute-start | bytes 2162696 | tf_op jit(solution)/vmap(transpose(jvp()))/dot_general | solution.py:9
  640.2 20.5 %collective-permute-start.23 = (f32[1,176,1024]{2,1,0:T(8,128)S(1)}, f32[1,176,1024]{2,1,0:T(8,128)S(1)}, u32[]{:S(2)}, u32[]{:S(2)}) collective-permute-start(f32[1,176,1024]{2,1,0:T(8,128)S(1)} %get-tuple-element.508), channel_id=46, source_target_pairs={{0,15},{1,0},{2,1},{3,2},{4,3},{5,4},{6,5},{7,6},{8,7},{9,8},{10,9... | collective-permute-start | bytes 2162696 | tf_op jit(solution)/vmap(transpose(jvp()))/dot_general | solution.py:9
  703.9 20.9 %collective-permute-start.20 = (f32[1,176,1024]{2,1,0:T(8,128)S(1)}, f32[1,176,1024]{2,1,0:T(8,128)S(1)}, u32[]{:S(2)}, u32[]{:S(2)}) collective-permute-start(f32[1,176,1024]{2,1,0:T(8,128)S(1)} %broadcast_select_fusion.34), channel_id=45, source_target_pairs={{0,1},{1,2},{2,3},{3,4},{4,5},{5,6},{6,7},{7,8},{8,9},{9,10},{10,1... | collective-permute-start | bytes 2162696 | tf_op jit(solution)/vmap(transpose(jvp()))/dot_general | solution.py:9
  725.1 20.8 %collective-permute-start.22 = (f32[1,176,1024]{2,1,0:T(8,128)S(1)}, f32[1,176,1024]{2,1,0:T(8,128)S(1)}, u32[]{:S(2)}, u32[]{:S(2)}) collective-permute-start(f32[1,176,1024]{2,1,0:T(8,128)S(1)} %get-tuple-element.507), channel_id=47, source_target_pairs={{0,1},{1,2},{2,3},{3,4},{4,5},{5,6},{6,7},{7,8},{8,9},{9,10},{10,1... | collective-permute-start | bytes 2162696 | tf_op jit(solution)/vmap(transpose(jvp()))/dot_general | solution.py:9
  725.1 20.7 %collective-permute-start.23 = (f32[1,176,1024]{2,1,0:T(8,128)S(1)}, f32[1,176,1024]{2,1,0:T(8,128)S(1)}, u32[]{:S(2)}, u32[]{:S(2)}) collective-permute-start(f32[1,176,1024]{2,1,0:T(8,128)S(1)} %get-tuple-element.508), channel_id=46, source_target_pairs={{0,15},{1,0},{2,1},{3,2},{4,3},{5,4},{6,5},{7,6},{8,7},{9,8},{10,9... | collective-permute-start | bytes 2162696 | tf_op jit(solution)/vmap(transpose(jvp()))/dot_general | solution.py:9
  748.1 20.8 %collective-permute-start.20 = (f32[1,176,1024]{2,1,0:T(8,128)S(1)}, f32[1,176,1024]{2,1,0:T(8,128)S(1)}, u32[]{:S(2)}, u32[]{:S(2)}) collective-permute-start(f32[1,176,1024]{2,1,0:T(8,128)S(1)} %broadcast_select_fusion.34), channel_id=45, source_target_pairs={{0,1},{1,2},{2,3},{3,4},{4,5},{5,6},{6,7},{7,8},{8,9},{9,10},{10,1... | collective-permute-start | bytes 2162696 | tf_op jit(solution)/vmap(transpose(jvp()))/dot_general | solution.py:9
  769.2 20.8 %collective-permute-start.22 = (f32[1,176,1024]{2,1,0:T(8,128)S(1)}, f32[1,176,1024]{2,1,0:T(8,128)S(1)}, u32[]{:S(2)}, u32[]{:S(2)}) collective-permute-start(f32[1,176,1024]{2,1,0:T(8,128)S(1)} %get-tuple-element.507), channel_id=47, source_target_pairs={{0,1},{1,2},{2,3},{3,4},{4,5},{5,6},{6,7},{7,8},{8,9},{9,10},{10,1... | collective-permute-start | bytes 2162696 | tf_op jit(solution)/vmap(transpose(jvp()))/dot_general | solution.py:9
  769.2 20.7 %collective-permute-start.23 = (f32[1,176,1024]{2,1,0:T(8,128)S(1)}, f32[1,176,1024]{2,1,0:T(8,128)S(1)}, u32[]{:S(2)}, u32[]{:S(2)}) collective-permute-start(f32[1,176,1024]{2,1,0:T(8,128)S(1)} %get-tuple-element.508), channel_id=46, source_target_pairs={{0,15},{1,0},{2,1},{3,2},{4,3},{5,4},{6,5},{7,6},{8,7},{9,8},{10,9... | collective-permute-start | bytes 2162696 | tf_op jit(solution)/vmap(transpose(jvp()))/dot_general | solution.py:9
  791.1 806.0 %collective-permute-start.29 = (f32[1,176,1024]{2,1,0:T(8,128)}, f32[1,176,1024]{2,1,0:T(8,128)}, u32[]{:S(2)}, u32[]{:S(2)}) collective-permute-start(f32[1,176,1024]{2,1,0:T(8,128)} %get-tuple-element.47), channel_id=48, source_target_pairs={{0,1},{1,2},{2,3},{3,4},{4,5},{5,6},{6,7},{7,8},{8,9},{9,10},{10,1... | collective-permute-start | bytes 2162696 | tf_op jit(solution)/vmap(transpose(jvp()))/dot_general | solution.py:9
  792.9 27.4 %collective-permute-start.8 = (f32[1,64,2816]{2,1,0:T(8,128)}, f32[1,64,2816]{2,1,0:T(8,128)}, u32[]{:S(2)}, u32[]{:S(2)}) collective-permute-start(f32[1,64,2816]{2,1,0:T(8,128)} %broadcast_select_fusion.28), channel_id=27, source_target_pairs={{0,1},{1,2},{2,3},{3,4},{4,5},{5,6},{6,7},{7,8},{8,9},{9,10},{10,1... | collective-permute-start | bytes 2162696 | tf_op jit(solution)/vmap(transpose(jvp()))/dot_general | solution.py:21
  793.8 26.5 %collective-permute-start.9 = (f32[1,64,2816]{2,1,0:T(8,128)}, f32[1,64,2816]{2,1,0:T(8,128)}, u32[]{:S(2)}, u32[]{:S(2)}) collective-permute-start(f32[1,64,2816]{2,1,0:T(8,128)} %broadcast_select_fusion.29), channel_id=26, source_target_pairs={{0,15},{1,0},{2,1},{3,2},{4,3},{5,4},{6,5},{7,6},{8,7},{9,8},{10,9... | collective-permute-start | bytes 2162696 | tf_op jit(solution)/vmap(transpose(jvp()))/dot_general | solution.py:21
  865.7 21.1 %collective-permute-start.10 = (f32[1,64,2816]{2,1,0:T(8,128)S(1)}, f32[1,64,2816]{2,1,0:T(8,128)S(1)}, u32[]{:S(2)}, u32[]{:S(2)}) collective-permute-start(f32[1,64,2816]{2,1,0:T(8,128)S(1)} %get-tuple-element.480), channel_id=29, source_target_pairs={{0,1},{1,2},{2,3},{3,4},{4,5},{5,6},{6,7},{7,8},{8,9},{9,10},{10,1... | collective-permute-start | bytes 2162696 | tf_op jit(solution)/vmap(transpose(jvp()))/dot_general | solution.py:21
  865.8 21.0 %collective-permute-start.11 = (f32[1,64,2816]{2,1,0:T(8,128)S(1)}, f32[1,64,2816]{2,1,0:T(8,128)S(1)}, u32[]{:S(2)}, u32[]{:S(2)}) collective-permute-start(f32[1,64,2816]{2,1,0:T(8,128)S(1)} %get-tuple-element.481), channel_id=28, source_target_pairs={{0,15},{1,0},{2,1},{3,2},{4,3},{5,4},{6,5},{7,6},{8,7},{9,8},{10,9... | collective-permute-start | bytes 2162696 | tf_op jit(solution)/vmap(transpose(jvp()))/dot_general | solution.py:21
  890.3 20.8 %collective-permute-start.8 = (f32[1,64,2816]{2,1,0:T(8,128)}, f32[1,64,2816]{2,1,0:T(8,128)}, u32[]{:S(2)}, u32[]{:S(2)}) collective-permute-start(f32[1,64,2816]{2,1,0:T(8,128)} %broadcast_select_fusion.28), channel_id=27, source_target_pairs={{0,1},{1,2},{2,3},{3,4},{4,5},{5,6},{6,7},{7,8},{8,9},{9,10},{10,1... | collective-permute-start | bytes 2162696 | tf_op jit(solution)/vmap(transpose(jvp()))/dot_general | solution.py:21
  977.7 617.0 %collective-permute-start.26 = (f32[1,64,2816]{2,1,0:T(8,128)}, f32[1,64,2816]{2,1,0:T(8,128)}, u32[]{:S(2)}, u32[]{:S(2)}) collective-permute-start(f32[1,64,2816]{2,1,0:T(8,128)} %get-tuple-element.41), channel_id=30, source_target_pairs={{0,1},{1,2},{2,3},{3,4},{4,5},{5,6},{6,7},{7,8},{8,9},{9,10},{10,1... | collective-permute-start | bytes 2162696 | tf_op jit(solution)/vmap(transpose(jvp()))/dot_general | solution.py:21
  1094.5 20.9 %collective-permute-start.12 = (f32[1,64,2816]{2,1,0:T(8,128)}, f32[1,64,2816]{2,1,0:T(8,128)}, u32[]{:S(2)}, u32[]{:S(2)}) collective-permute-start(f32[1,64,2816]{2,1,0:T(8,128)} %broadcast_select_fusion.30), channel_id=33, source_target_pairs={{0,1},{1,2},{2,3},{3,4},{4,5},{5,6},{6,7},{7,8},{8,9},{9,10},{10,1... | collective-permute-start | bytes 2162696 | tf_op jit(solution)/vmap(transpose(jvp()))/dot_general | solution.py:21
  1139.5 21.1 %collective-permute-start.12 = (f32[1,64,2816]{2,1,0:T(8,128)}, f32[1,64,2816]{2,1,0:T(8,128)}, u32[]{:S(2)}, u32[]{:S(2)}) collective-permute-start(f32[1,64,2816]{2,1,0:T(8,128)} %broadcast_select_fusion.30), channel_id=33, source_target_pairs={{0,1},{1,2},{2,3},{3,4},{4,5},{5,6},{6,7},{7,8},{8,9},{9,10},{10,1... | collective-permute-start | bytes 2162696 | tf_op jit(solution)/vmap(transpose(jvp()))/dot_general | solution.py:21
  1184.1 20.7 %collective-permute-start.12 = (f32[1,64,2816]{2,1,0:T(8,128)}, f32[1,64,2816]{2,1,0:T(8,128)}, u32[]{:S(2)}, u32[]{:S(2)}) collective-permute-start(f32[1,64,2816]{2,1,0:T(8,128)} %broadcast_select_fusion.30), channel_id=33, source_target_pairs={{0,1},{1,2},{2,3},{3,4},{4,5},{5,6},{6,7},{7,8},{8,9},{9,10},{10,1... | collective-permute-start | bytes 2162696 | tf_op jit(solution)/vmap(transpose(jvp()))/dot_general | solution.py:21
  1593.3 21.3 %collective-permute-start.25 = (f32[1,64,2816]{2,1,0:T(8,128)}, f32[1,64,2816]{2,1,0:T(8,128)S(1)}, u32[]{:S(2)}, u32[]{:S(2)}) collective-permute-start(f32[1,64,2816]{2,1,0:T(8,128)} %get-tuple-element.39), channel_id=24, source_target_pairs={{0,1},{1,2},{2,3},{3,4},{4,5},{5,6},{6,7},{7,8},{8,9},{9,10},{10,1... | collective-permute-start | bytes 2162696 | tf_op jit(solution)/vmap(transpose(jvp()))/dot_general | solution.py:20
  (163 other events, 3420.2 us)
Sparse Core Ops, SparseCore 0:
  10.3 58.9 all-gather.29
  71.6 57.3 all-gather.31
  131.3 57.3 all-gather.33
  190.8 57.3 all-gather.35
  250.3 57.3 all-gather.39
  309.9 57.3 all-gather.37
where the time goes:
time: 1630 us; the launch traced here: 1620 us
  waiting for transfers between devices  644 us (40%)
  matrix products  452 us (28%)
  starting transfers between devices  215 us (13%)
  other arithmetic  158 us (10%)
  local copies, waits for them, and re-layouts  87.5 us (5%)
  loops' own time  51.1 us (3%)
    squeeze x6, waiting for transfers between devices, stack(): h = layer(h, {name: w[number] for name, w in weights.items()})  174 us
    dot_general x34, waiting for transfers between devices, layer(): gate = jnp.dot(a, w['w_gate'], preferred_element_type=jnp.float32)  158 us
    dot_general x19, matrix products, matmul(): jnp.dot(a, w, preferred_element_type=jnp.float32).astype(jnp.bfloat16)  157 us
    dot_general x34, waiting for transfers between devices, layer(): up = jnp.dot(a, w['w_up'], preferred_element_type=jnp.float32)  156 us
    dot_general x20, matrix products, layer(): up = jnp.dot(a, w['w_up'], preferred_element_type=jnp.float32)  156 us
    dot_general x34, waiting for transfers between devices, matmul(): jnp.dot(a, w, preferred_element_type=jnp.float32).astype(jnp.bfloat16)  155 us
    dot_general x20, matrix products, layer(): gate = jnp.dot(a, w['w_gate'], preferred_element_type=jnp.float32)  140 us
    dot_general x64, other arithmetic  72.4 us
  transfers between devices with their start and end apart: 108, of which 57 were waited for; matrix products, arithmetic and copies ran while one was open for 43% of the time, Pallas kernels for 0%

commit v1 on v0

v1 whole, which is shorter than its diff:
```python
import functools

import jax
import jax.numpy as jnp
from jax import lax
from jax.experimental import pallas as pl
from jax.experimental.pallas import tpu as pltpu
from jax.sharding import Mesh, PartitionSpec as P


F32, BF16 = jnp.float32, jnp.bfloat16
SWAP = [(0, 1), (1, 0)]
CHIPS = 8
ANY = pl.BlockSpec(memory_space=pl.ANY)


def dot(a, b, ca, cb):
    return lax.dot_general(a, b, (((ca,), (cb,)), ((), ())), preferred_element_type=F32)


def at(q):
    q = q % CHIPS
    return jnp.where(q < CHIPS // 2, q, CHIPS + CHIPS // 2 - 1 - q)


def place(q):
    q = q % CHIPS
    return q if q < CHIPS // 2 else CHIPS + CHIPS // 2 - 1 - q


RIGHT = [(place(q), place(q + 1)) for q in range(CHIPS)]
LEFT = [(place(q + 1), place(q)) for q in range(CHIPS)]
STEPS = {False: (4, 3), True: (3, 4)}


def offsets(flip):
    left, right = STEPS[flip]
    return [0] + [-j for j in range(1, left + 1)] + [j for j in range(1, right + 1)]


class Gather:
    def __init__(self, piece, flip):
        self.way = [[piece], [piece]]
        self.flip = flip
        self.sib = {}
        self.swap()

    def swap(self):
        for i, way in enumerate(self.way):
            for j in range(min(i, 1), len(way)):
                if (i, j) not in self.sib:
                    self.sib[i, j] = lax.ppermute(way[j], "core", SWAP)

    def step(self):
        old = [len(w) for w in self.way]
        for i, (steps, to) in enumerate(zip(STEPS[self.flip], (RIGHT, LEFT))):
            if old[i] <= steps:
                self.way[i].append(lax.ppermute(self.way[i][-1], "yz", to))

    def pieces(self):
        keys = [(0, j) for j in range(len(self.way[0]))] + [(1, j) for j in range(1, len(self.way[1]))]
        return [self.way[i][j] for i, j in keys], [self.sib[key] for key in keys]


class Scatter:
    def __init__(self, terms, p, flip):
        self.terms, self.p = lax.optimization_barrier((terms, p))
        self.left = list(STEPS[flip])
        self.came = [None, None]

    def step(self):
        for i, (way, sign) in enumerate(((RIGHT, 1), (LEFT, -1))):
            j = self.left[i]
            if j:
                p, came, terms = self.p, self.came[i], self.terms
                if came is not None:
                    p, came, terms = lax.optimization_barrier((p, came, terms))
                send = lax.dynamic_index_in_dim(terms, at(p + sign * j + CHIPS), 0, False)
                if came is not None:
                    send = send + came.astype(F32)
                self.came[i] = lax.ppermute(send.astype(BF16), "yz", way)
                self.left[i] -= 1

    def result(self):
        assert self.left == [0, 0]
        p, terms, *came = lax.optimization_barrier((self.p, self.terms, *self.came))
        total = lax.dynamic_index_in_dim(terms, at(p), 0, False)
        for t in came:
            total = total + t.astype(F32)
        return total.astype(BF16)


def cost(flops, *arrays):
    return pl.CostEstimate(
        flops=int(flops), bytes_accessed=int(sum(a.size * a.dtype.itemsize for a in arrays)), transcendentals=0
    )


class Weight:
    def __init__(self, pieces, shape):
        self.own, self.sib = pieces
        self.shape = shape

    @property
    def operands(self):
        return [*self.own, *self.sib]

    def copies(self, refs, meta, table, whole, sem):
        c = meta[0]
        out = []
        rows, half = refs[0].shape[1:]
        for number, ref in enumerate(refs):
            side = c if number < CHIPS else 1 - c
            chip = meta[1 + table * CHIPS + number % CHIPS]
            col = pl.multiple_of(side * half, 128)
            for k in range(2):
                core = side if k == 0 else 1 - side
                row = pl.multiple_of((2 * chip + core) * rows, 16)
                out.append(pltpu.make_async_copy(ref.at[k], whole.at[pl.ds(row, rows), pl.ds(col, half)], sem))
        return out


def with_weights(body, weights, tables, meta, grid, in_specs, ins, out_specs, out_shape, scratch, flops, prior=()):
    n_in, n_out = len(ins), len(out_shape)

    def kernel(meta_ref, *refs):
        at_in, refs = refs[:n_in], refs[n_in:]
        at_w = []
        for _ in weights:
            at_w.append(refs[: 2 * CHIPS])
            refs = refs[2 * CHIPS :]
        refs = refs[len(prior) :]
        outs, refs = refs[:n_out], refs[n_out:]
        wholes, refs = refs[: len(weights)], refs[len(weights) :]
        sem, rest = refs[0], refs[1:]
        first = functools.reduce(jnp.logical_and, [pl.program_id(i) == 0 for i in range(len(grid))])

        @pl.when(first)
        def _():
            copies = []
            for w, r, whole, table in zip(weights, at_w, wholes, tables):
                copies += w.copies(r, meta_ref, table, whole, sem)
            for t in copies:
                t.start()
            for t in copies:
                t.wait()

        body(at_in, outs, wholes, rest)

    operands = [t for w in weights for t in w.operands]
    return pl.pallas_call(
        kernel,
        out_shape=out_shape,
        grid_spec=pltpu.PrefetchScalarGridSpec(
            num_scalar_prefetch=1,
            grid=grid,
            in_specs=list(in_specs) + [ANY] * (len(operands) + len(prior)),
            out_specs=out_specs,
            scratch_shapes=[pltpu.VMEM(w.shape, BF16) for w in weights] + [pltpu.SemaphoreType.DMA] + list(scratch),
        ),
        cost_estimate=cost(flops, *ins, *operands, *out_shape),
        input_output_aliases={1 + n_in + len(operands) + i: i for i in range(len(prior))},
        compiler_params=pltpu.CompilerParams(dimension_semantics=("arbitrary",) * len(grid)),
    )(meta, *ins, *operands, *prior)


def solution(mesh):
    groups, size = mesh.shape["rep"], mesh.shape["dp"]
    mine = Mesh(mesh.devices.reshape(groups, size // 2, 2), ("rep", "yz", "core"))

    def step(x, dy, w_gate, w_up, w_down):
        x, dy = x[0], dy[0]
        layers, rows, ff = w_gate.shape
        tokens, d = x.shape
        fh, dh_ = ff // 2, d // 2
        c = lax.axis_index("core")
        k = lax.axis_index("yz")
        p = jnp.where(k < CHIPS // 2, k, CHIPS + CHIPS // 2 - 1 - k)
        meta = jnp.stack([c] + [at(p + o + CHIPS) for f in (False, True) for o in offsets(f)]).astype(jnp.int32)

        both = jnp.stack([w_gate, w_up], 1).reshape(layers * 2, rows, ff)
        take = lambda t, side, n: lax.dynamic_slice_in_dim(t, side * n, n, -1)
        gu = jnp.stack([take(both, c, fh), lax.ppermute(take(both, 1 - c, fh), "core", SWAP)], 1)
        dn = jnp.stack([take(w_down, c, dh_), lax.ppermute(take(w_down, 1 - c, dh_), "core", SWAP)], 1)
        gathers = {}
        for l in range(layers):
            gathers.update({f"g{l}": Gather(gu[2 * l], False), f"u{l}": Gather(gu[2 * l + 1], True), f"d{l}": Gather(dn[l], bool(l))})

        wg, wu, wd = [None] * 2, [None] * 2, [None] * 2

        tm = tokens // 2
        tn = 256
        tile = lambda r, n, o=0: pl.BlockSpec((r, n), lambda i, *_: (i + o, 0))
        cell = lambda o=0: pl.BlockSpec((tm, tn), lambda i, j, *_: (i + o, j))
        one = 2 * tokens * d * ff

        def normed(wide):
            return (wide * lax.rsqrt(jnp.mean(wide * wide, -1, keepdims=True) + 1e-6)).astype(BF16)

        def columns():
            return pl.ds(pl.multiple_of(pl.program_id(1) * tn, tn), tn)

        def gate_up(a, l, part, prior):
            def body(ins, outs, ws, _):
                n = columns()
                g = dot(ins[0][...], ws[0][:, n], 1, 0)
                u = dot(ins[0][...], ws[1][:, n], 1, 0)
                outs[0][...] = g
                outs[1][...] = u
                outs[2][...] = (g * jax.nn.sigmoid(g) * u).astype(BF16)

            shape = lambda t: jax.ShapeDtypeStruct((tokens, ff), t)
            return with_weights(
                body, [wg[l], wu[l]], [0, 1], meta, (1, ff // tn), [tile(tm, d, part)], [a],
                [cell(part)] * 3, [shape(F32), shape(F32), shape(BF16)], [], one, prior,
            )

        def d_gate_up(d_act, g, u):
            sig = jax.nn.sigmoid(g)
            return (d_act * u * (sig * (1 + g * (1 - sig)))).astype(BF16), (d_act * (g * sig)).astype(BF16)

        def last(a, d_act, l):
            def body(ins, outs, ws, _):
                n = columns()
                g = dot(ins[0][...], ws[0][:, n], 1, 0)
                u = dot(ins[0][...], ws[1][:, n], 1, 0)
                d_act = ins[1][...].astype(F32)
                outs[0][...] = (g * jax.nn.sigmoid(g) * u).astype(BF16)
                outs[1][...], outs[2][...] = d_gate_up(d_act, g, u)

            return with_weights(
                body, [wg[l], wu[l]], [0, 1], meta, (tokens // tm, ff // tn), [tile(tm, d), cell()], [a, d_act],
                [cell()] * 3, [jax.ShapeDtypeStruct((tokens, ff), BF16)] * 3, [], 2 * one,
            )

        def d_act_of(dh, l):
            def body(ins, outs, ws, _):
                outs[0][...] = dot(ins[0][...], ws[0][columns(), :], 1, 1).astype(BF16)

            return with_weights(
                body, [wd[l]], [l], meta, (tokens // tm, ff // tn), [tile(tm, d)], [dh],
                [cell()], [jax.ShapeDtypeStruct((tokens, ff), BF16)], [], one,
            )[0]

        def d_hidden(dh, gate, up, l):
            def body(ins, outs, ws, _):
                d_act = dot(ins[0][...], ws[0][columns(), :], 1, 1).astype(BF16).astype(F32)
                outs[0][...], outs[1][...] = d_gate_up(d_act, ins[1][...], ins[2][...])

            return with_weights(
                body, [wd[l]], [l], meta, (tokens // tm, ff // tn), [tile(tm, d), cell(), cell()], [dh, gate, up],
                [cell()] * 2, [jax.ShapeDtypeStruct((tokens, ff), BF16)] * 2, [], one,
            )

        tt = tokens // 4

        def down(act, h, l):
            def body(ins, outs, ws, _):
                out = dot(ins[0][...], ws[0][...], 1, 0).astype(BF16)
                new = (ins[1][...].astype(F32) + out.astype(F32)).astype(BF16)
                outs[0][...] = new
                outs[1][...] = normed(new.astype(F32))

            return with_weights(
                body, [wd[l]], [l], meta, (tokens // tt,), [tile(tt, ff), tile(tt, d)], [act, h],
                [tile(tt, d)] * 2, [jax.ShapeDtypeStruct((tokens, d), BF16)] * 2, [], one,
            )

        def back(d_gate, d_up, h, dh, l, part, prior):
            def body(ins, outs, ws, _):
                da = dot(ins[0][...], ws[0][...], 1, 1) + dot(ins[1][...], ws[1][...], 1, 1)
                da = da.astype(BF16).astype(F32)
                wide = ins[2][...].astype(F32)
                inv = lax.rsqrt(jnp.mean(wide * wide, -1, keepdims=True) + 1e-6)
                proj = jnp.mean(da * wide, -1, keepdims=True) * (inv * inv * inv)
                term = (da * inv - wide * proj).astype(BF16).astype(F32)
                outs[0][...] = (ins[3][...].astype(F32) + term).astype(BF16)

            return with_weights(
                body, [wg[l], wu[l]], [0, 1], meta, (2,), [tile(tt, ff, 2 * part)] * 2 + [tile(tt, d, 2 * part)] * 2,
                [d_gate, d_up, h, dh], [tile(tt, d, 2 * part)], [jax.ShapeDtypeStruct((tokens, d), BF16)], [], one, prior,
            )

        def outer(a, b, came):
            m, half = a.shape[1], b.shape[1] // 2
            tk = min(512, tokens)
            steps = tokens // tk
            own = came is not None

            def kernel(meta_ref, a_ref, b_ref, *refs):
                i = pl.program_id(0)
                if own:
                    came_ref, out, got, sem = refs
                    acc = out
                    copy = pltpu.make_async_copy(came_ref, got, sem)

                    @pl.when(i == 0)
                    def _():
                        copy.start()
                else:
                    out, acc = refs
                t = dot(a_ref[...], b_ref[...], 0, 0)

                @pl.when(i == 0)
                def _():
                    acc[...] = t

                @pl.when(i > 0)
                def _():
                    acc[...] += t

                @pl.when(i == steps - 1)
                def _():
                    if own:
                        copy.wait()
                        out[...] += got[...].astype(F32)
                    else:
                        out[...] = acc[...].astype(BF16)

            whole = pl.BlockSpec((m, half), lambda i, meta: (0, 0))
            side = (lambda meta: meta[0]) if own else (lambda meta: 1 - meta[0])
            out = jax.ShapeDtypeStruct((m, half), F32 if own else BF16)
            extra = [came] if own else []
            return pl.pallas_call(
                kernel,
                out_shape=out,
                grid_spec=pltpu.PrefetchScalarGridSpec(
                    num_scalar_prefetch=1,
                    grid=(steps,),
                    in_specs=[
                        pl.BlockSpec((tk, m), lambda i, meta: (i, 0)),
                        pl.BlockSpec((tk, half), lambda i, meta: (i, side(meta))),
                    ] + [ANY] * len(extra),
                    out_specs=whole,
                    scratch_shapes=[pltpu.VMEM((m, half), BF16), pltpu.SemaphoreType.DMA] if own else [pltpu.VMEM((m, half), F32)],
                ),
                cost_estimate=cost(one // 2, a, out, *extra, *extra),
                compiler_params=pltpu.CompilerParams(dimension_semantics=("arbitrary",)),
            )(meta, a, b, *extra)

        def keep(total):
            t = total.reshape(2, -1, total.shape[-1])
            here = lax.dynamic_index_in_dim(t, c, 0, False)
            came = lax.ppermute(lax.dynamic_index_in_dim(t, 1 - c, 0, False), "core", SWAP)
            return jnp.concatenate([jnp.where(c == 0, here, came), jnp.where(c == 0, came, here)], -1)

        rings = dict(gathers)

        def slot(names, work):
            for name in names.split():
                rings[name].step()
            return work() if work else None

        def gathered(l, *names):
            for name in names:
                gathers[name].swap()
                shape = (ff, d) if name[0] == "d" else (d, ff)
                {"g": wg, "u": wu, "d": wd}[name[0]][l] = Weight(gathers[name].pieces(), shape)

        def move(*names):
            for name in names:
                gathers[name].swap()

        def send(half):
            return lax.ppermute(half, "core", SWAP)

        def ring(name, own, flip):
            rings[name] = Scatter(own.reshape(CHIPS, -1, own.shape[-1]), p, flip)

        h0 = x
        a0 = normed(x.astype(F32))
        for _ in range(4):
            slot("g0 u0", None)
            move("g0", "u0")
        gathered(0, "g0", "u0")
        first = slot("d0 d1", lambda: gate_up(a0, 0, 0, ()))
        move("d0", "d1")
        gate0, up0, act0 = slot("d0 d1", lambda: gate_up(a0, 0, 1, first))
        for _ in range(2):
            move("d0", "d1")
            slot("d0 d1", None)
        gathered(0, "d0")
        gathered(1, "d1")
        h1, a1 = slot("g1 u1", lambda: down(act0, h0, 0))
        move("g1", "u1")
        d_act1 = slot("g1 u1", lambda: d_act_of(dy, 1))
        for _ in range(2):
            move("g1", "u1")
            slot("g1 u1", None)
        gathered(1, "g1", "u1")
        act1, dg1, du1 = last(a1, d_act1, 1)

        d1s = send(outer(act1, dy, None))
        g1s = send(outer(a1, dg1, None))
        ring("d1", outer(act1, dy, d1s), False)
        g1, u1s = slot("d1", lambda: (outer(a1, dg1, g1s), send(outer(a1, du1, None))))
        ring("g1", g1, True)
        first, u1 = slot("d1 g1", lambda: (back(dg1, du1, h1, dy, 1, 0, ()), outer(a1, du1, u1s)))
        ring("u1", u1, False)
        (dh1,) = slot("d1 g1 u1", lambda: back(dg1, du1, h1, dy, 1, 1, first))
        d0s, dg0, du0 = slot("d1 g1 u1", lambda: (send(outer(act0, dh1, None)), *d_hidden(dh1, gate0, up0, 0)))
        d0, g0s = slot("g1 u1", lambda: (outer(act0, dh1, d0s), send(outer(a0, dg0, None))))
        ring("d0", d0, True)
        g0, u0s = slot("u1 d0", lambda: (outer(a0, dg0, g0s), send(outer(a0, du0, None))))
        ring("g0", g0, False)
        u0 = slot("d0 g0", lambda: outer(a0, du0, u0s))
        ring("u0", u0, True)
        first = slot("d0 g0 u0", lambda: back(dg0, du0, h0, dh1, 0, 0, ()))
        (dx,) = slot("d0 g0 u0", lambda: back(dg0, du0, h0, dh1, 0, 1, first))
        slot("g0 u0", None)
        slot("u0", None)
        done = {name: keep(r.result()) for name, r in rings.items()}
        out = [jnp.stack([done[n + "0"], done[n + "1"]]) for n in "gud"]
        return dx[None], *out

    device = ("yz", "core")
    weight = P(None, device, None)
    seq = P(("rep",) + device, None, None)
    grad = P("rep", device, None)
    return jax.shard_map(
        step, mesh=mine, in_specs=(seq, seq, weight, weight, weight), out_specs=(seq, grad, grad, grad), check_vma=False
    )
```

time: 1630 us -> 816 us (0.50)
  waiting for transfers between devices: 644 us -> 156 us
  matrix products: 452 us -> 0 us
  Pallas kernels: 0 us -> 442 us
  starting transfers between devices: 215 us -> 105 us
  other arithmetic: 158 us -> 77.3 us
  local copies, waits for them, and re-layouts: 87.5 us -> 21.4 us
  loops' own time: 51.1 us -> 0 us
    dot_general x102 -> x0, waiting for transfers between devices: 469 us -> none  [the longest x34 158 us: layer(): gate = jnp.dot(a, w['w_gate'], preferred_element_type=jnp.float32)]
    dot_general x59 -> x0, matrix products: 452 us -> none  [the longest x19 157 us: matmul(): jnp.dot(a, w, preferred_element_type=jnp.float32).astype(jnp.bfloat16)]
    pallas_call x0 -> x22, Pallas kernels: none -> 442 us  [the longest x10 272 us: with_weights(): pl.pallas_call(kernel, out_shape=out_shape, grid_spec=pltpu.PrefetchScala...]
    dot_general x102 -> x0, starting transfers between devices: 215 us -> none  [the longest x34 72 us: matmul(): jnp.dot(a, w, preferred_element_type=jnp.float32).astype(jnp.bfloat16)]
    squeeze x6 -> x0, waiting for transfers between devices: 174 us -> none  [stack(): h = layer(h, {name: w[number] for name, w in weights.items()})]
    ppermute x0 -> x146, waiting for transfers between devices: none -> 156 us  [the longest x42 117 us: step(): self.way[i].append(lax.ppermute(self.way[i][-1], 'yz', to))]
    dot_general x112 -> x0, other arithmetic: 127 us -> none
    ppermute x0 -> x146, starting transfers between devices: none -> 105 us  [the longest x42 47.8 us: step(): self.way[i].append(lax.ppermute(self.way[i][-1], 'yz', to))]
  transfers between devices with their start and end apart: 108 -> 146, of which waited for: 57 -> 42; matrix products, arithmetic and copies ran while one was open for 43% -> 11% of each run, Pallas kernels for 0% -> 48%
where the time goes in v1:
time: 816 us; the launch traced here: 804 us
  Pallas kernels  442 us (54%)
  waiting for transfers between devices  156 us (19%)
  starting transfers between devices  105 us (13%)
  other arithmetic  77.3 us (9%)
  local copies, waits for them, and re-layouts  21.4 us (3%)
    pallas_call x10, Pallas kernels, with_weights(): pl.pallas_call(kernel, out_shape=out_shape, grid_spec=pltpu.PrefetchScala...  272 us
    pallas_call x12, Pallas kernels, outer(): pl.pallas_call(kernel, out_shape=out, grid_spec=pltpu.PrefetchScalarGridS...  170 us
    ppermute x42, waiting for transfers between devices, step(): self.way[i].append(lax.ppermute(self.way[i][-1], 'yz', to))  117 us
    convert_element_type x30, other arithmetic, step(): self.came[i] = lax.ppermute(send.astype(BF16), 'yz', way)  53.7 us
    ppermute x42, starting transfers between devices, step(): self.way[i].append(lax.ppermute(self.way[i][-1], 'yz', to))  47.8 us
    ppermute x42, starting transfers between devices, step(): self.came[i] = lax.ppermute(send.astype(BF16), 'yz', way)  46.3 us
    ppermute x42, waiting for transfers between devices, step(): self.came[i] = lax.ppermute(send.astype(BF16), 'yz', way)  36.8 us
  transfers between devices with their start and end apart: 146, of which 42 were waited for; matrix products, arithmetic and copies ran while one was open for 11% of the time, Pallas kernels for 48%

profile of v1, /device:TPU:6, one launch (start us, length us, event | category | flops | bytes accessed | tf_op | source)
XLA Modules:
  0.0 804.0 jit_solution(13831833064117039700)
XLA Ops:
  20.2 5.8 collective-permute-done.50.refs_5_
  61.4 5.7 collective-permute-done.62.refs_3_.refs_5_
  93.2 6.8 collective-permute-done.34.refs_5_.refs_6_
  113.5 5.5 collective-permute-done.63.refs_4_.refs_6_
  120.4 6.1 collective-permute-done.67.refs_8_.refs_10_
  130.7 7.1 collective-permute-done.3.refs_4_.refs_7_
  139.5 7.0 collective-permute-done.7.refs_8_.refs_11_
  149.4 7.9 collective-permute-done.35.refs_6_.refs_7_
  164.7 5.7 collective-permute-done.64.refs_5_.refs_7_
  181.4 24.6 %shard_map.87.refs_1_ = bf16[2048,2816]{1,0:T(8,128)(2,1)} custom-call(s32[17]{0:T(128)} %stack.104.meta_ref, bf16[2048,1024]{1,0:T(8,128)(2,1)} %bitcast.273, bf16[2,176,512]{2,1,0:T(8,128)(2,1)} %copy-done.57, bf16[2,176,512]{2,1,0:T(8,128)(2,1)} %collective-permute-done.47.refs_2_, bf16[2,176,512]{2,1,0:T(8,128)(2,1)} %copy-done.76, ...), custom_call_target="tpu_custom_call" | custom-call | flops 11811160064 | bytes 21495808 | tf_op jit(solution)/shard_map/pallas_call | solution.py:151
  209.8 23.7 %shard_map.84 = (f32[2048,2816]{1,0:T(8,128)}, f32[2048,2816]{1,0:T(8,128)}, bf16[2048,2816]{1,0:T(8,128)(2,1)}) custom-call(s32[17]{0:T(128)} %stack.104.meta_ref, bf16[2048,1024]{1,0:T(8,128)(2,1)} %fusion.1.refs_0_.a_ref, bf16[2,64,1408]{2,1,0:T(8,128)(2,1)} %copy-done.1, bf16[2,64,1408]{2,1,0:T(8,128)(2,1)} %copy-done.5, ...), custom_call_target="tpu_custom_call" | custom-call | flops 11811160064 | bytes 73400320 | tf_op jit(solution)/shard_map/pallas_call | solution.py:151
  236.1 23.7 %shard_map.85 = (f32[2048,2816]{1,0:T(8,128)}, f32[2048,2816]{1,0:T(8,128)}, bf16[2048,2816]{1,0:T(8,128)(2,1)}) custom-call(s32[17]{0:T(128)} %stack.104.meta_ref, bf16[2048,1024]{1,0:T(8,128)(2,1)} %fusion.1.refs_0_.a_ref, bf16[2,64,1408]{2,1,0:T(8,128)(2,1)} %copy-done.1, ...), custom_call_target="tpu_custom_call", output_to_operand_aliasing={{0}: (34, {}), {1}: (35, {}), {2}: (36, {})} | custom-call | flops 11811160064 | bytes 73400320 | tf_op jit(solution)/shard_map/pallas_call | solution.py:151
  261.8 20.8 %shard_map.86 = (bf16[2048,1024]{1,0:T(8,128)(2,1)}, bf16[2048,1024]{1,0:T(8,128)(2,1)}) custom-call(s32[17]{0:T(128)} %stack.104.meta_ref, bf16[2048,2816]{1,0:T(8,128)(2,1)} %get-tuple-element.146.refs_0_.a_ref, bf16[2048,1024]{1,0:T(8,128)(2,1)} %bitcast.270, bf16[2,176,512]{2,1,0:T(8,128)(2,1)} %copy-done.54, bf16[2,176,512]{2,1,0:T(8,128)(2,1)} %copy-done.66, ...), custom_call_target="tpu_custom_call" | custom-call | flops 11811160064 | bytes 29884416 | tf_op jit(solution)/shard_map/pallas_call | solution.py:151
  283.7 44.0 %shard_map.88 = (bf16[2048,2816]{1,0:T(8,128)(2,1)}, bf16[2048,2816]{1,0:T(8,128)(2,1)}, bf16[2048,2816]{1,0:T(8,128)(2,1)}) custom-call(s32[17]{0:T(128)} %stack.104.meta_ref, bf16[2048,1024]{1,0:T(8,128)(2,1)} %get-tuple-element.147.refs_0_.a_ref, bf16[2048,2816]{1,0:T(8,128)(2,1)} %shard_map.87.refs_1_, bf16[2,64,1408]{2,1,0:T(8,128)(2,1)} %copy-done.4, ...), custom_call_target="tpu_custom_call" | custom-call | flops 23622320128 | bytes 61865984 | tf_op jit(solution)/shard_map/pallas_call | solution.py:151
  327.7 13.4 %shard_map.104 = bf16[2816,512]{1,0:T(8,128)(2,1)} custom-call(s32[17]{0:T(128)} %stack.104.meta_ref, bf16[2048,2816]{1,0:T(8,128)(2,1)} %get-tuple-element.260.a_ref, bf16[2048,1024]{1,0:T(8,128)(2,1)} %bitcast.274), custom_call_target="tpu_custom_call" | custom-call | flops 5905580032 | bytes 14417920 | tf_op jit(solution)/shard_map/pallas_call | solution.py:324
  341.2 13.6 %shard_map.100 = bf16[1024,1408]{1,0:T(8,128)(2,1)} custom-call(s32[17]{0:T(128)} %stack.104.meta_ref, bf16[2048,1024]{1,0:T(8,128)(2,1)} %get-tuple-element.147.refs_0_.a_ref, bf16[2048,2816]{1,0:T(8,128)(2,1)} %get-tuple-element.149.refs_1_.b_ref), custom_call_target="tpu_custom_call" | custom-call | flops 5905580032 | bytes 7077888 | tf_op jit(solution)/shard_map/pallas_call | solution.py:324
  354.7 24.2 %shard_map.89.refs_36_ = bf16[2048,1024]{1,0:T(8,128)(2,1)} custom-call(s32[17]{0:T(128)} %stack.104.meta_ref, bf16[2048,2816]{1,0:T(8,128)(2,1)} %get-tuple-element.148.refs_0_.b_ref, bf16[2048,2816]{1,0:T(8,128)(2,1)} %get-tuple-element.149.refs_1_.b_ref, bf16[2048,1024]{1,0:T(8,128)(2,1)} %get-tuple-element.150.refs_2_, bf16[2048,1024]{1,0:T(8,128)(2,1)} %bitcast.275, ...), custom_call_target="tpu_custom_call" | custom-call | flops 11811160064 | bytes 47185920 | tf_op jit(solution)/shard_map/pallas_call | solution.py:151
  378.9 24.1 %shard_map.90.refs_0_.refs_3_.b_ref = bf16[2048,1024]{1,0:T(8,128)(2,1)} custom-call(s32[17]{0:T(128)} %stack.104.meta_ref, bf16[2048,2816]{1,0:T(8,128)(2,1)} %get-tuple-element.148.refs_0_.b_ref, bf16[2048,2816]{1,0:T(8,128)(2,1)} %get-tuple-element.149.refs_1_.b_ref, ...), custom_call_target="tpu_custom_call", output_to_operand_aliasing={{}: (37, {})} | custom-call | flops 11811160064 | bytes 47185920 | tf_op jit(solution)/shard_map/pallas_call | solution.py:151
  403.0 13.4 %shard_map.102 = bf16[2816,512]{1,0:T(8,128)(2,1)} custom-call(s32[17]{0:T(128)} %stack.104.meta_ref, bf16[2048,2816]{1,0:T(8,128)(2,1)} %get-tuple-element.146.refs_0_.a_ref, bf16[2048,1024]{1,0:T(8,128)(2,1)} %shard_map.90.refs_0_.refs_3_.b_ref), custom_call_target="tpu_custom_call" | custom-call | flops 5905580032 | bytes 14417920 | tf_op jit(solution)/shard_map/pallas_call | solution.py:324
  417.0 39.4 %shard_map.91 = (bf16[2048,2816]{1,0:T(8,128)(2,1)}, bf16[2048,2816]{1,0:T(8,128)(2,1)}) custom-call(s32[17]{0:T(128)} %stack.104.meta_ref, bf16[2048,1024]{1,0:T(8,128)(2,1)} %shard_map.90.refs_0_.refs_3_.b_ref, f32[2048,2816]{1,0:T(8,128)} %get-tuple-element.151.refs_1_, f32[2048,2816]{1,0:T(8,128)} %get-tuple-element.152.refs_2_, ...), custom_call_target="tpu_custom_call" | custom-call | flops 11811160064 | bytes 79167488 | tf_op jit(solution)/shard_map/pallas_call | solution.py:151
  456.4 13.7 %shard_map.98 = bf16[1024,1408]{1,0:T(8,128)(2,1)} custom-call(s32[17]{0:T(128)} %stack.104.meta_ref, bf16[2048,1024]{1,0:T(8,128)(2,1)} %fusion.1.refs_0_.a_ref, bf16[2048,2816]{1,0:T(8,128)(2,1)} %get-tuple-element.154.refs_1_.b_ref), custom_call_target="tpu_custom_call" | custom-call | flops 5905580032 | bytes 7077888 | tf_op jit(solution)/shard_map/pallas_call | solution.py:324
  470.5 13.6 %shard_map.96 = bf16[1024,1408]{1,0:T(8,128)(2,1)} custom-call(s32[17]{0:T(128)} %stack.104.meta_ref, bf16[2048,1024]{1,0:T(8,128)(2,1)} %get-tuple-element.147.refs_0_.a_ref, bf16[2048,2816]{1,0:T(8,128)(2,1)} %get-tuple-element.148.refs_0_.b_ref), custom_call_target="tpu_custom_call" | custom-call | flops 5905580032 | bytes 7077888 | tf_op jit(solution)/shard_map/pallas_call | solution.py:324
  484.2 13.6 %shard_map.94 = bf16[1024,1408]{1,0:T(8,128)(2,1)} custom-call(s32[17]{0:T(128)} %stack.104.meta_ref, bf16[2048,1024]{1,0:T(8,128)(2,1)} %fusion.1.refs_0_.a_ref, bf16[2048,2816]{1,0:T(8,128)(2,1)} %get-tuple-element.153.refs_0_.b_ref), custom_call_target="tpu_custom_call" | custom-call | flops 5905580032 | bytes 7077888 | tf_op jit(solution)/shard_map/pallas_call | solution.py:324
  498.2 14.5 %shard_map.105 = f32[2816,512]{1,0:T(8,128)} custom-call(s32[17]{0:T(128)} %stack.104.meta_ref, bf16[2048,2816]{1,0:T(8,128)(2,1)} %get-tuple-element.260.a_ref, bf16[2048,1024]{1,0:T(8,128)(2,1)} %bitcast.277, bf16[2816,512]{1,0:T(8,128)(2,1)} %collective-permute-done.137.refs_0_), custom_call_target="tpu_custom_call" | custom-call | flops 5905580032 | bytes 23068672 | tf_op jit(solution)/shard_map/pallas_call | solution.py:324
  512.7 14.9 %shard_map.103 = f32[2816,512]{1,0:T(8,128)} custom-call(s32[17]{0:T(128)} %stack.104.meta_ref, bf16[2048,2816]{1,0:T(8,128)(2,1)} %get-tuple-element.146.refs_0_.a_ref, bf16[2048,1024]{1,0:T(8,128)(2,1)} %shard_map.90.refs_0_.refs_3_.b_ref, bf16[2816,512]{1,0:T(8,128)(2,1)} %collective-permute-done.128.refs_0_), custom_call_target="tpu_custom_call" | custom-call | flops 5905580032 | bytes 23068672 | tf_op jit(solution)/shard_map/pallas_call | solution.py:324
  527.7 14.7 %shard_map.101 = f32[1024,1408]{1,0:T(8,128)} custom-call(s32[17]{0:T(128)} %stack.104.meta_ref, bf16[2048,1024]{1,0:T(8,128)(2,1)} %get-tuple-element.147.refs_0_.a_ref, bf16[2048,2816]{1,0:T(8,128)(2,1)} %get-tuple-element.149.refs_1_.b_ref, bf16[1024,1408]{1,0:T(8,128)(2,1)} %collective-permute-done.119.refs_0_), custom_call_target="tpu_custom_call" | custom-call | flops 5905580032 | bytes 15728640 | tf_op jit(solution)/shard_map/pallas_call | solution.py:324
  551.7 14.7 %shard_map.99 = f32[1024,1408]{1,0:T(8,128)} custom-call(s32[17]{0:T(128)} %stack.104.meta_ref, bf16[2048,1024]{1,0:T(8,128)(2,1)} %fusion.1.refs_0_.a_ref, bf16[2048,2816]{1,0:T(8,128)(2,1)} %get-tuple-element.154.refs_1_.b_ref, bf16[1024,1408]{1,0:T(8,128)(2,1)} %collective-permute-done.110.refs_0_), custom_call_target="tpu_custom_call" | custom-call | flops 5905580032 | bytes 15728640 | tf_op jit(solution)/shard_map/pallas_call | solution.py:324
  567.0 14.6 %shard_map.97 = f32[1024,1408]{1,0:T(8,128)} custom-call(s32[17]{0:T(128)} %stack.104.meta_ref, bf16[2048,1024]{1,0:T(8,128)(2,1)} %get-tuple-element.147.refs_0_.a_ref, bf16[2048,2816]{1,0:T(8,128)(2,1)} %get-tuple-element.148.refs_0_.b_ref, bf16[1024,1408]{1,0:T(8,128)(2,1)} %collective-permute-done.101.refs_0_), custom_call_target="tpu_custom_call" | custom-call | flops 5905580032 | bytes 15728640 | tf_op jit(solution)/shard_map/pallas_call | solution.py:324
  583.3 14.8 %shard_map.95 = f32[1024,1408]{1,0:T(8,128)} custom-call(s32[17]{0:T(128)} %stack.104.meta_ref, bf16[2048,1024]{1,0:T(8,128)(2,1)} %fusion.1.refs_0_.a_ref, bf16[2048,2816]{1,0:T(8,128)(2,1)} %get-tuple-element.153.refs_0_.b_ref, bf16[1024,1408]{1,0:T(8,128)(2,1)} %copy-done.29), custom_call_target="tpu_custom_call" | custom-call | flops 5905580032 | bytes 15728640 | tf_op jit(solution)/shard_map/pallas_call | solution.py:324
  668.0 24.0 %shard_map.92.refs_36_ = bf16[2048,1024]{1,0:T(8,128)(2,1)} custom-call(s32[17]{0:T(128)} %stack.104.meta_ref, bf16[2048,2816]{1,0:T(8,128)(2,1)} %get-tuple-element.153.refs_0_.b_ref, bf16[2048,2816]{1,0:T(8,128)(2,1)} %get-tuple-element.154.refs_1_.b_ref, bf16[2048,1024]{1,0:T(8,128)(2,1)} %bitcast.271, ...), custom_call_target="tpu_custom_call" | custom-call | flops 11811160064 | bytes 47185920 | tf_op jit(solution)/shard_map/pallas_call | solution.py:151
  746.7 5.7 collective-permute-done.141
  761.3 24.0 %shard_map.93 = bf16[2048,1024]{1,0:T(8,128)(2,1)} custom-call(s32[17]{0:T(128)} %stack.104.meta_ref, bf16[2048,2816]{1,0:T(8,128)(2,1)} %get-tuple-element.153.refs_0_.b_ref, bf16[2048,2816]{1,0:T(8,128)(2,1)} %get-tuple-element.154.refs_1_.b_ref, bf16[2048,1024]{1,0:T(8,128)(2,1)} %bitcast.272, ...), custom_call_target="tpu_custom_call", output_to_operand_aliasing={{}: (37, {})} | custom-call | flops 11811160064 | bytes 47185920 | tf_op jit(solution)/shard_map/pallas_call | solution.py:151
  (514 shorter events, 296.0 us)
Async XLA Ops:
  175.4 30.7 %collective-permute-start.29 = (bf16[2,64,1408]{2,1,0:T(8,128)(2,1)}, bf16[2,64,1408]{2,1,0:T(8,128)(2,1)S(1)}, u32[]{:S(2)}, u32[]{:S(2)}) collective-permute-start(bf16[2,64,1408]{2,1,0:T(8,128)(2,1)} %collective-permute-done.21.refs_23_.refs_26_), channel_id=1, source_target_pairs={{0,1},{1,0},{2,3},{3,2},{4,5},{5,4},{6,7},{7,6},{8,9},{9,8},{10,11... | collective-permute-start | bytes 1081352 | tf_op jit(solution)/shard_map/ppermute | solution.py:52
  177.1 29.1 %collective-permute-start.15 = (bf16[2,64,1408]{2,1,0:T(8,128)(2,1)}, bf16[2,64,1408]{2,1,0:T(8,128)(2,1)S(1)}, u32[]{:S(2)}, u32[]{:S(2)}) collective-permute-start(bf16[2,64,1408]{2,1,0:T(8,128)(2,1)} %collective-permute-done.7.refs_8_.refs_11_), channel_id=1, source_target_pairs={{0,1},{1,0},{2,3},{3,2},{4,5},{5,4},{6,7},{7,6},{8,9},{9,8},{10,11... | collective-permute-start | bytes 1081352 | tf_op jit(solution)/shard_map/ppermute | solution.py:52
  180.2 26.6 %collective-permute-start.26 = (bf16[2,64,1408]{2,1,0:T(8,128)(2,1)}, bf16[2,64,1408]{2,1,0:T(8,128)(2,1)S(1)}, u32[]{:S(2)}, u32[]{:S(2)}) collective-permute-start(bf16[2,64,1408]{2,1,0:T(8,128)(2,1)} %collective-permute-done.18.refs_20_.refs_23_), channel_id=1, source_target_pairs={{0,1},{1,0},{2,3},{3,2},{4,5},{5,4},{6,7},{7,6},{8,9},{9,8},{10,11... | collective-permute-start | bytes 1081352 | tf_op jit(solution)/shard_map/ppermute | solution.py:52
  180.2 26.8 %collective-permute-start.12 = (bf16[2,64,1408]{2,1,0:T(8,128)(2,1)}, bf16[2,64,1408]{2,1,0:T(8,128)(2,1)S(1)}, u32[]{:S(2)}, u32[]{:S(2)}) collective-permute-start(bf16[2,64,1408]{2,1,0:T(8,128)(2,1)} %collective-permute-done.4.refs_5_.refs_8_), channel_id=1, source_target_pairs={{0,1},{1,0},{2,3},{3,2},{4,5},{5,4},{6,7},{7,6},{8,9},{9,8},{10,11... | collective-permute-start | bytes 1081352 | tf_op jit(solution)/shard_map/ppermute | solution.py:52
  180.7 28.3 %collective-permute-start.30 = (bf16[2,64,1408]{2,1,0:T(8,128)(2,1)}, bf16[2,64,1408]{2,1,0:T(8,128)(2,1)S(1)}, u32[]{:S(2)}, u32[]{:S(2)}) collective-permute-start(bf16[2,64,1408]{2,1,0:T(8,128)(2,1)} %collective-permute-done.22.refs_24_.refs_27_), channel_id=1, source_target_pairs={{0,1},{1,0},{2,3},{3,2},{4,5},{5,4},{6,7},{7,6},{8,9},{9,8},{10,11... | collective-permute-start | bytes 1081352 | tf_op jit(solution)/shard_map/ppermute | solution.py:52
  206.1 29.0 %collective-permute-start.71 = (bf16[2,64,1408]{2,1,0:T(8,128)(2,1)}, bf16[2,64,1408]{2,1,0:T(8,128)(2,1)}, u32[]{:S(2)}, u32[]{:S(2)}) collective-permute-start(bf16[2,64,1408]{2,1,0:T(8,128)(2,1)} %collective-permute-done.63.refs_4_.refs_6_), channel_id=1, source_target_pairs={{0,1},{1,0},{2,3},{3,2},{4,5},{5,4},{6,7},{7,6},{8,9},{9,8},{10,11... | collective-permute-start | bytes 1081352 | tf_op jit(solution)/shard_map/ppermute | solution.py:52
  206.2 27.2 %collective-permute-start.68 = (bf16[2,64,1408]{2,1,0:T(8,128)(2,1)S(1)}, bf16[2,64,1408]{2,1,0:T(8,128)(2,1)}, u32[]{:S(2)}, u32[]{:S(2)}) collective-permute-start(bf16[2,64,1408]{2,1,0:T(8,128)(2,1)S(1)} %copy-done.37), channel_id=1, source_target_pairs={{2,0},{4,2},{6,4},{14,6},{12,14},{10,12},{8,10},{0,8},{3,1},{5,3},... | collective-permute-start | bytes 1081352 | tf_op jit(solution)/shard_map/ppermute | solution.py:58
  206.7 28.6 %collective-permute-start.75 = (bf16[2,64,1408]{2,1,0:T(8,128)(2,1)S(1)}, bf16[2,64,1408]{2,1,0:T(8,128)(2,1)}, u32[]{:S(2)}, u32[]{:S(2)}) collective-permute-start(bf16[2,64,1408]{2,1,0:T(8,128)(2,1)S(1)} %copy-done.37), channel_id=1, source_target_pairs={{0,1},{1,0},{2,3},{3,2},{4,5},{5,4},{6,7},{7,6},{8,9},{9,8},{10,11... | collective-permute-start | bytes 1081352 | tf_op jit(solution)/shard_map/ppermute | solution.py:52
  206.9 26.6 %collective-permute-start.79 = (bf16[2,64,1408]{2,1,0:T(8,128)(2,1)S(1)}, bf16[2,64,1408]{2,1,0:T(8,128)(2,1)}, u32[]{:S(2)}, u32[]{:S(2)}) collective-permute-start(bf16[2,64,1408]{2,1,0:T(8,128)(2,1)S(1)} %copy-done.39), channel_id=1, source_target_pairs={{0,2},{2,4},{4,6},{6,14},{14,12},{12,10},{10,8},{8,0},{1,3},{3,5},... | collective-permute-start | bytes 1081352 | tf_op jit(solution)/shard_map/ppermute | solution.py:58
  209.0 26.6 %collective-permute-start.86 = (bf16[2,64,1408]{2,1,0:T(8,128)(2,1)S(1)}, bf16[2,64,1408]{2,1,0:T(8,128)(2,1)}, u32[]{:S(2)}, u32[]{:S(2)}) collective-permute-start(bf16[2,64,1408]{2,1,0:T(8,128)(2,1)S(1)} %copy-done.39), channel_id=1, source_target_pairs={{0,1},{1,0},{2,3},{3,2},{4,5},{5,4},{6,7},{7,6},{8,9},{9,8},{10,11... | collective-permute-start | bytes 1081352 | tf_op jit(solution)/shard_map/ppermute | solution.py:52
  233.6 27.2 %collective-permute-start.65 = (bf16[2,64,1408]{2,1,0:T(8,128)(2,1)}, bf16[2,64,1408]{2,1,0:T(8,128)(2,1)S(1)}, u32[]{:S(2)}, u32[]{:S(2)}) collective-permute-start(bf16[2,64,1408]{2,1,0:T(8,128)(2,1)} %collective-permute-done.64.refs_5_.refs_7_), channel_id=1, source_target_pairs={{0,2},{2,4},{4,6},{6,14},{14,12},{12,10},{10,8},{8,0},{1,3},{3,5},... | collective-permute-start | bytes 1081352 | tf_op jit(solution)/shard_map/ppermute | solution.py:58
  341.1 156.7 %collective-permute-start.137 = (bf16[2816,512]{1,0:T(8,128)(2,1)}, bf16[2816,512]{1,0:T(8,128)(2,1)}, u32[]{:S(2)}, u32[]{:S(2)}) collective-permute-start(bf16[2816,512]{1,0:T(8,128)(2,1)} %shard_map.104), channel_id=1, source_target_pairs={{0,1},{1,0},{2,3},{3,2},{4,5},{5,4},{6,7},{7,6},{8,9},{9,8},{10,11... | collective-permute-start | bytes 8650760 | tf_op jit(solution)/shard_map/ppermute | solution.py:365
  416.5 96.3 %collective-permute-start.128 = (bf16[2816,512]{1,0:T(8,128)(2,1)}, bf16[2816,512]{1,0:T(8,128)(2,1)}, u32[]{:S(2)}, u32[]{:S(2)}) collective-permute-start(bf16[2816,512]{1,0:T(8,128)(2,1)} %shard_map.102), channel_id=1, source_target_pairs={{0,1},{1,0},{2,3},{3,2},{4,5},{5,4},{6,7},{7,6},{8,9},{9,8},{10,11... | collective-permute-start | bytes 8650760 | tf_op jit(solution)/shard_map/ppermute | solution.py:365
  416.9 110.8 %collective-permute-start.119 = (bf16[1024,1408]{1,0:T(8,128)(2,1)}, bf16[1024,1408]{1,0:T(8,128)(2,1)}, u32[]{:S(2)}, u32[]{:S(2)}) collective-permute-start(bf16[1024,1408]{1,0:T(8,128)(2,1)} %shard_map.100), channel_id=1, source_target_pairs={{0,1},{1,0},{2,3},{3,2},{4,5},{5,4},{6,7},{7,6},{8,9},{9,8},{10,11... | collective-permute-start | bytes 8650760 | tf_op jit(solution)/shard_map/ppermute | solution.py:365
  470.1 81.2 %collective-permute-start.110 = (bf16[1024,1408]{1,0:T(8,128)(2,1)}, bf16[1024,1408]{1,0:T(8,128)(2,1)}, u32[]{:S(2)}, u32[]{:S(2)}) collective-permute-start(bf16[1024,1408]{1,0:T(8,128)(2,1)} %shard_map.98), channel_id=1, source_target_pairs={{0,1},{1,0},{2,3},{3,2},{4,5},{5,4},{6,7},{7,6},{8,9},{9,8},{10,11... | collective-permute-start | bytes 8650760 | tf_op jit(solution)/shard_map/ppermute | solution.py:365
  484.1 82.3 %collective-permute-start.101 = (bf16[1024,1408]{1,0:T(8,128)(2,1)}, bf16[1024,1408]{1,0:T(8,128)(2,1)}, u32[]{:S(2)}, u32[]{:S(2)}) collective-permute-start(bf16[1024,1408]{1,0:T(8,128)(2,1)} %shard_map.96), channel_id=1, source_target_pairs={{0,1},{1,0},{2,3},{3,2},{4,5},{5,4},{6,7},{7,6},{8,9},{9,8},{10,11... | collective-permute-start | bytes 8650760 | tf_op jit(solution)/shard_map/ppermute | solution.py:365
  497.8 83.8 %collective-permute-start.92 = (bf16[1024,1408]{1,0:T(8,128)(2,1)}, bf16[1024,1408]{1,0:T(8,128)(2,1)S(1)}, u32[]{:S(2)}, u32[]{:S(2)}) collective-permute-start(bf16[1024,1408]{1,0:T(8,128)(2,1)} %shard_map.94), channel_id=1, source_target_pairs={{0,1},{1,0},{2,3},{3,2},{4,5},{5,4},{6,7},{7,6},{8,9},{9,8},{10,11... | collective-permute-start | bytes 8650760 | tf_op jit(solution)/shard_map/ppermute | solution.py:365
  544.8 54.9 %collective-permute-start.142 = (bf16[352,512]{1,0:T(8,128)(2,1)}, bf16[352,512]{1,0:T(8,128)(2,1)}, u32[]{:S(2)}, u32[]{:S(2)}) collective-permute-start(bf16[352,512]{1,0:T(8,128)(2,1)} %get-tuple-element.284), channel_id=1, source_target_pairs={{2,0},{4,2},{6,4},{14,6},{12,14},{10,12},{8,10},{0,8},{3,1},{5,3},... | collective-permute-start | bytes 1081352 | tf_op jit(solution)/shard_map/ppermute | solution.py:81
  545.2 57.1 %collective-permute-start.138 = (bf16[352,512]{1,0:T(8,128)(2,1)}, bf16[352,512]{1,0:T(8,128)(2,1)}, u32[]{:S(2)}, u32[]{:S(2)}) collective-permute-start(bf16[352,512]{1,0:T(8,128)(2,1)} %get-tuple-element.285), channel_id=1, source_target_pairs={{0,2},{2,4},{4,6},{6,14},{14,12},{12,10},{10,8},{8,0},{1,3},{3,5},... | collective-permute-start | bytes 1081352 | tf_op jit(solution)/shard_map/ppermute | solution.py:81
  551.2 52.6 %collective-permute-start.132 = (bf16[352,512]{1,0:T(8,128)(2,1)}, bf16[352,512]{1,0:T(8,128)(2,1)}, u32[]{:S(2)}, u32[]{:S(2)}) collective-permute-start(bf16[352,512]{1,0:T(8,128)(2,1)} %get-tuple-element.282), channel_id=1, source_target_pairs={{2,0},{4,2},{6,4},{14,6},{12,14},{10,12},{8,10},{0,8},{3,1},{5,3},... | collective-permute-start | bytes 1081352 | tf_op jit(solution)/shard_map/ppermute | solution.py:81
  566.5 37.9 %collective-permute-start.124 = (bf16[128,1408]{1,0:T(8,128)(2,1)}, bf16[128,1408]{1,0:T(8,128)(2,1)}, u32[]{:S(2)}, u32[]{:S(2)}) collective-permute-start(bf16[128,1408]{1,0:T(8,128)(2,1)} %get-tuple-element.288), channel_id=1, source_target_pairs={{2,0},{4,2},{6,4},{14,6},{12,14},{10,12},{8,10},{0,8},{3,1},{5,3},... | collective-permute-start | bytes 1081352 | tf_op jit(solution)/shard_map/ppermute | solution.py:81
  581.6 26.6 %collective-permute-start.120 = (bf16[128,1408]{1,0:T(8,128)(2,1)}, bf16[128,1408]{1,0:T(8,128)(2,1)}, u32[]{:S(2)}, u32[]{:S(2)}) collective-permute-start(bf16[128,1408]{1,0:T(8,128)(2,1)} %get-tuple-element.289), channel_id=1, source_target_pairs={{0,2},{2,4},{4,6},{6,14},{14,12},{12,10},{10,8},{8,0},{1,3},{3,5},... | collective-permute-start | bytes 1081352 | tf_op jit(solution)/shard_map/ppermute | solution.py:81
  613.6 39.9 %collective-permute-start.129 = (bf16[352,512]{1,0:T(8,128)(2,1)S(1)}, bf16[352,512]{1,0:T(8,128)(2,1)}, u32[]{:S(2)}, u32[]{:S(2)}) collective-permute-start(bf16[352,512]{1,0:T(8,128)(2,1)S(1)} %get-tuple-element.283), channel_id=1, source_target_pairs={{0,2},{2,4},{4,6},{6,14},{14,12},{12,10},{10,8},{8,0},{1,3},{3,5},... | collective-permute-start | bytes 1081352 | tf_op jit(solution)/shard_map/ppermute | solution.py:81
  657.4 36.6 %collective-permute-start.112 = (bf16[128,1408]{1,0:T(8,128)(2,1)}, bf16[128,1408]{1,0:T(8,128)(2,1)S(1)}, u32[]{:S(2)}, u32[]{:S(2)}) collective-permute-start(bf16[128,1408]{1,0:T(8,128)(2,1)} %fusion.29), channel_id=1, source_target_pairs={{0,2},{2,4},{4,6},{6,14},{14,12},{12,10},{10,8},{8,0},{1,3},{3,5},... | collective-permute-start | bytes 1081352 | tf_op jit(solution)/shard_map/ppermute | solution.py:81
  657.9 37.8 %collective-permute-start.106 = (bf16[128,1408]{1,0:T(8,128)(2,1)}, bf16[128,1408]{1,0:T(8,128)(2,1)S(1)}, u32[]{:S(2)}, u32[]{:S(2)}) collective-permute-start(bf16[128,1408]{1,0:T(8,128)(2,1)} %fusion.34), channel_id=1, source_target_pairs={{2,0},{4,2},{6,4},{14,6},{12,14},{10,12},{8,10},{0,8},{3,1},{5,3},... | collective-permute-start | bytes 1081352 | tf_op jit(solution)/shard_map/ppermute | solution.py:81
  659.5 36.2 %collective-permute-start.103 = (bf16[128,1408]{1,0:T(8,128)(2,1)}, bf16[128,1408]{1,0:T(8,128)(2,1)S(1)}, u32[]{:S(2)}, u32[]{:S(2)}) collective-permute-start(bf16[128,1408]{1,0:T(8,128)(2,1)} %fusion.36), channel_id=1, source_target_pairs={{0,2},{2,4},{4,6},{6,14},{14,12},{12,10},{10,8},{8,0},{1,3},{3,5},... | collective-permute-start | bytes 1081352 | tf_op jit(solution)/shard_map/ppermute | solution.py:81
  664.8 30.9 %collective-permute-start.98 = (bf16[128,1408]{1,0:T(8,128)(2,1)}, bf16[128,1408]{1,0:T(8,128)(2,1)S(1)}, u32[]{:S(2)}, u32[]{:S(2)}) collective-permute-start(bf16[128,1408]{1,0:T(8,128)(2,1)} %fusion.40), channel_id=1, source_target_pairs={{2,0},{4,2},{6,4},{14,6},{12,14},{10,12},{8,10},{0,8},{3,1},{5,3},... | collective-permute-start | bytes 1081352 | tf_op jit(solution)/shard_map/ppermute | solution.py:81
  666.4 29.3 %collective-permute-start.94 = (bf16[128,1408]{1,0:T(8,128)(2,1)}, bf16[128,1408]{1,0:T(8,128)(2,1)S(1)}, u32[]{:S(2)}, u32[]{:S(2)}) collective-permute-start(bf16[128,1408]{1,0:T(8,128)(2,1)} %fusion.43), channel_id=1, source_target_pairs={{0,2},{2,4},{4,6},{6,14},{14,12},{12,10},{10,8},{8,0},{1,3},{3,5},... | collective-permute-start | bytes 1081352 | tf_op jit(solution)/shard_map/ppermute | solution.py:81
  744.7 40.7 %collective-permute-start.104 = (bf16[128,1408]{1,0:T(8,128)(2,1)S(1)}, bf16[128,1408]{1,0:T(8,128)(2,1)S(1)}, u32[]{:S(2)}, u32[]{:S(2)}) collective-permute-start(bf16[128,1408]{1,0:T(8,128)(2,1)S(1)} %fusion.35), channel_id=1, source_target_pairs={{0,2},{2,4},{4,6},{6,14},{14,12},{12,10},{10,8},{8,0},{1,3},{3,5},... | collective-permute-start | bytes 1081352 | tf_op jit(solution)/shard_map/ppermute | solution.py:81
  745.8 39.6 %collective-permute-start.99 = (bf16[128,1408]{1,0:T(8,128)(2,1)S(1)}, bf16[128,1408]{1,0:T(8,128)(2,1)S(1)}, u32[]{:S(2)}, u32[]{:S(2)}) collective-permute-start(bf16[128,1408]{1,0:T(8,128)(2,1)S(1)} %fusion.39), channel_id=1, source_target_pairs={{2,0},{4,2},{6,4},{14,6},{12,14},{10,12},{8,10},{0,8},{3,1},{5,3},... | collective-permute-start | bytes 1081352 | tf_op jit(solution)/shard_map/ppermute | solution.py:81
  752.4 32.9 %collective-permute-start.117 = (bf16[128,1408]{1,0:T(8,128)(2,1)}, bf16[128,1408]{1,0:T(8,128)(2,1)}, u32[]{:S(2)}, u32[]{:S(2)}) collective-permute-start(bf16[128,1408]{1,0:T(8,128)(2,1)} %fusion.25), channel_id=1, source_target_pairs={{2,0},{4,2},{6,4},{14,6},{12,14},{10,12},{8,10},{0,8},{3,1},{5,3},... | collective-permute-start | bytes 1081352 | tf_op jit(solution)/shard_map/ppermute | solution.py:81
  752.9 32.5 %collective-permute-start.108 = (bf16[128,1408]{1,0:T(8,128)(2,1)}, bf16[128,1408]{1,0:T(8,128)(2,1)}, u32[]{:S(2)}, u32[]{:S(2)}) collective-permute-start(bf16[128,1408]{1,0:T(8,128)(2,1)} %fusion.32), channel_id=1, source_target_pairs={{2,0},{4,2},{6,4},{14,6},{12,14},{10,12},{8,10},{0,8},{3,1},{5,3},... | collective-permute-start | bytes 1081352 | tf_op jit(solution)/shard_map/ppermute | solution.py:81
  (195 other events, 5343.9 us)
